TPU v7x, 512 devices: a whole 4x8x8 slice. The times are simulated.
512 devices in a mesh: row: 4 (over x), col: 4 (over z_lo), depth: 32 (over y, z_hi, core).
Axes of the slice: x: 4, y: 8, z: 8 (z_hi: 2, z_lo: 4; z = z_hi * 4 + z_lo), core: 2. Of those that a mesh axis runs over, the one named last changes fastest.
Arguments:
- orbitals: bfloat16 [2, 1024, 32, 4096], P(None, ('row', 'col'), 'depth'), may hold values from -20 to 20
- potential: float32 [32, 4096], P('depth'), may hold values from -6 to 6
Outputs:
- intersection: float32 [1024, 2, 1024], P(('row', 'depth'), None, 'col')
- applied: bfloat16 [2, 1024, 32, 4096], P(None, ('row', 'col'), 'depth')
All inputs are finite; a program needn't handle non-finite values.
Results may differ from a plain program's by a relative error of at most 0.001.
Values may be sent and summed in bfloat16 or wider, within the bound.
No kernel may reach another device: no remote copies, remote signals or barrier semaphores. Data moves between devices by JAX's collectives and lax.ppermute only.
A program may use at most 128 MiB of HBM per device.

v0:
```python
import jax
import jax.numpy as jnp
from jax import lax
from jax.sharding import PartitionSpec as P

NX = 64


def sent_to_all(x, axis):
    copies = jnp.broadcast_to(x, (lax.axis_size(axis), *x.shape))
    return lax.all_to_all(copies, axis, split_axis=0, concat_axis=0, tiled=True)


def in_order(pieces, dim):
    lengths = list(pieces.shape[1:])
    lengths[dim] *= pieces.shape[0]
    return jnp.moveaxis(pieces, 0, dim).reshape(lengths)


def gathered_copies(x, axis, dim):
    pieces = sent_to_all(x, axis)
    return in_order(pieces, dim)


def with_halo(block, sides, width):
    for axis, dim in sides:
        count = lax.axis_size(axis)
        forward = [(i, i + 1) for i in range(count - 1)]
        forward.append((count - 1, 0))
        backward = [(target, source) for source, target in forward]
        low = lax.ppermute(
            lax.slice_in_dim(block, block.shape[dim] - width, None, axis=dim), axis, forward
        )
        high = lax.ppermute(lax.slice_in_dim(block, 0, width, axis=dim), axis, backward)
        block = jnp.concatenate([low, block, high], axis=dim)
    return block


def cut_along(x, dim, size):
    before, after = (x.shape[:dim], x.shape[dim + 1 :])
    return jnp.moveaxis(x.reshape(*before, size, -1, *after), dim, 0)


def sum_at_owner(x, axis, dim):
    size = lax.axis_size(axis)
    pieces = lax.all_to_all(cut_along(x, dim, size), axis, 0, 0, tiled=True)
    return jnp.sum(pieces, axis=0)


def apply_operator(padded, potential):
    center = padded[:, :, 1:-1].astype(jnp.float32)
    below = padded[:, :, :-2].astype(jnp.float32)
    above = padded[:, :, 2:].astype(jnp.float32)
    flat_cells = center.shape[-1]
    xpos = jnp.arange(flat_cells) % NX
    yminus = jnp.roll(center, NX, axis=3)
    yplus = jnp.roll(center, -NX, axis=3)
    xminus = jnp.where(xpos == 0, jnp.roll(center, 1 - NX, axis=3), jnp.roll(center, 1, axis=3))
    xplus = jnp.where(
        xpos == NX - 1, jnp.roll(center, NX - 1, axis=3), jnp.roll(center, -1, axis=3)
    )
    lap = below + above + yminus + yplus + xminus + xplus - 6.0 * center
    return (-0.5 * lap + potential[None, None] * center).astype(jnp.bfloat16)


def contract(left, right):
    return lax.dot_general(
        left, right, (((1,), (1,)), ((), ())), preferred_element_type=jnp.float32
    )


def shards(orbitals, potential):
    parts, orbs, planes, cells = orbitals.shape
    flat = orbitals.reshape(parts, orbs, planes * cells)
    panel = lax.all_gather(flat, "col", axis=1, tiled=True)
    other = gathered_copies(flat, "row", 1)
    padded = with_halo(orbitals, (("depth", 2),), 1)
    applied = apply_operator(padded, potential)
    dvol = 1.0 / (planes * lax.axis_size("depth") * cells)
    tile_cols = other.shape[1]
    real_rows = panel[0]
    imag_rows = panel[1]
    sreal = contract(real_rows, other[0]) + contract(imag_rows, other[1])
    simag = contract(real_rows, other[1]) - contract(imag_rows, other[0])
    summed = sum_at_owner(dvol * jnp.concatenate([sreal, simag], axis=1), "depth", 0)
    intersection = summed.reshape(summed.shape[0], 2, tile_cols)
    intersection = lax.all_to_all(intersection, "col", split_axis=2, concat_axis=2, tiled=True)
    return (intersection, applied)


def solution(mesh):
    in_specs = (P(None, ("row", "col"), "depth", None), P("depth", None))
    out_specs = (P(("row", "depth"), None, "col"), P(None, ("row", "col"), "depth", None))
    return jax.shard_map(shards, mesh=mesh, in_specs=in_specs, out_specs=out_specs, check_vma=False)
```

profile of v0, /device:TPU:10, one launch (start us, length us, event | category | flops | bytes accessed | tf_op | source)
XLA Modules:
  0.0 205.3 jit_solution(4994023229630989519)
XLA Ops:
  7.2 0.0 all-gather.3.cloned.1.call-start
  7.2 0.7 all-gather.3.cloned.1.call-update
  7.9 3.7 %broadcast_in_dim.11 = bf16[4,2,64,4096]{3,2,1,0:T(8,128)(2,1)} broadcast(bf16[2,64,4096]{2,1,0:T(8,128)(2,1)} %bitcast.31), dimensions={1,2,3} | broadcast | bytes 5242880 | tf_op jit(solution)/shard_map/broadcast_in_dim | solution.py:10
  11.6 0.0 copy-start
  11.6 5.5 %all-to-all-start = ((bf16[4,2,64,4096]{3,2,1,0:T(8,128)(2,1)}), bf16[4,2,64,4096]{3,2,1,0:T(8,128)(2,1)}, u32[]{:S(2)}, u32[]{:S(2)}) async-start(bf16[4,2,64,4096]{3,2,1,0:T(8,128)(2,1)} %broadcast_in_dim.11), calls=%async_computation | async-start | bytes 8388608 | tf_op jit(solution)/shard_map/all_to_all | solution.py:11
  17.1 0.0 copy-done
  17.1 1.9 collective-permute-start
  19.0 10.0 %collective-permute-start.1 = (bf16[2,64,1,4096]{3,1,2,0:T(8,128)(2,1)S(1)}, bf16[2,64,1,4096]{3,1,2,0:T(8,128)(2,1)}, u32[]{:S(2)}, u32[]{:S(2)}) collective-permute-start(bf16[2,64,1,4096]{3,1,2,0:T(8,128)(2,1)S(1)} %copy-done), channel_id=1, source_target_pairs={{1,0},{2,1},{3,2},{4,3},{5,4},{6,5},{7,6},{8,7},{9,8},{10,9},{11,1... | collective-permute-start | bytes 3145736 | tf_op jit(solution)/shard_map/ppermute | solution.py:34
  29.0 0.6 fusion.17
  29.6 0.1 fusion.26
  29.7 0.7 fusion.23
  30.4 0.7 fusion.22
  31.1 1.8 fusion.24
  32.9 2.4 %fusion.25 = (f32[2,64,1,4032]{3,1,2,0:T(8,128)}, f32[2,64,1,4032]{3,1,2,0:T(8,128)}) fusion(bf16[2,64,1,4096]{3,1,2,0:T(8,128)(2,1)S(1)} %copy-done), kind=kLoop, calls=%fused_computation.33 | loop fusion | bytes 8257536 | tf_op jit(solution)/shard_map/jit(_roll_static)/slice | solution.py:57
  35.3 29.5 %all-to-all-done = bf16[4,2,64,4096]{3,2,1,0:T(8,128)(2,1)} async-done(((bf16[4,2,64,4096]{3,2,1,0:T(8,128)(2,1)}), bf16[4,2,64,4096]{3,2,1,0:T(8,128)(2,1)}, u32[]{:S(2)}, u32[]{:S(2)}) %all-to-all-start) | async-done | bytes 4194336 | tf_op jit(solution)/shard_map/all_to_all | solution.py:11
  64.8 4.7 %fusion.20 = (bf16[1,4,64,4096]{3,2,0,1:T(8,128)(2,1)}, bf16[1,4,64,4096]{3,2,0,1:T(8,128)(2,1)}) fusion(bf16[2,4,64,4096]{3,2,0,1:T(8,128)(2,1)} %bitcast.2), kind=kLoop, calls=%fused_computation.28 | loop fusion | bytes 8388608 | tf_op jit(solution)/shard_map/slice | solution.py:83
  69.5 74.9 %all-gather.3.cloned.1.call-done = bf16[2,256,1,4096]{3,1,2,0:T(8,128)(2,1)} async-done(((bf16[2,64,1,4096]{3,1,2,0:T(8,128)(2,1)}), bf16[2,256,1,4096]{3,1,2,0:T(8,128)(2,1)}) %all-gather.3.cloned.1.call-update) | async-done | bytes 4194320 | tf_op jit(solution)/shard_map/all_gather | solution.py:75
  144.4 0.0 copy-start.2
  144.4 3.1 %fusion.7 = f32[256,256]{1,0:T(8,128)S(1)} fusion(bf16[256,4096]{1,0:T(8,128)(2,1)} %bitcast.32, bf16[2,256,1,4096]{3,1,2,0:T(8,128)(2,1)} %all-gather.3.cloned.1.call-done), kind=kOutput, calls=%fused_computation.12 | convolution fusion | flops 536870912 | bytes 4456448 | tf_op jit(solution)/shard_map/dot_general | solution.py:67
  147.5 0.0 copy-done.2
  147.5 0.0 copy-start.3
  147.5 2.5 %fusion.8 = f32[256,256]{1,0:T(8,128)S(1)} fusion(bf16[256,4096]{1,0:T(8,128)(2,1)S(1)} %bitcast.34, bf16[2,256,1,4096]{3,1,2,0:T(8,128)(2,1)} %all-gather.3.cloned.1.call-done), kind=kOutput, calls=%fused_computation.13 | convolution fusion | flops 536870912 | bytes 4456448 | tf_op jit(solution)/shard_map/dot_general | solution.py:67
  150.0 0.3 copy-done.3
  150.4 0.0 copy-start.1
  150.4 0.7 fusion.14
  151.1 0.8 copy-done.1
  151.9 0.7 fusion.12
  152.7 0.9 maximum_multiply_fusion
  153.6 9.2 %all-to-all-start.1 = ((f32[32,8,512]{2,1,0:T(8,128)}), f32[32,8,512]{2,1,0:T(8,128)}, u32[]{:S(2)}, u32[]{:S(2)}) async-start(f32[32,8,512]{2,1,0:T(8,128)} %maximum_multiply_fusion), calls=%async_computation.1 | async-start | bytes 1048576 | tf_op jit(solution)/shard_map/all_to_all | solution.py:46
  162.8 2.4 %fusion.21 = (f32[2,64,1,4095]{3,1,2,0:T(8,128)}, f32[2,64,1,4095]{3,1,2,0:T(8,128)}) fusion(bf16[2,64,1,4096]{3,1,2,0:T(8,128)(2,1)S(1)} %copy-done), kind=kLoop, calls=%fused_computation.29 | loop fusion | bytes 8386560 | tf_op jit(solution)/shard_map/jit(_roll_static)/slice | solution.py:60
  165.2 17.6 %all-to-all-done.1 = f32[32,8,512]{2,1,0:T(8,128)} async-done(((f32[32,8,512]{2,1,0:T(8,128)}), f32[32,8,512]{2,1,0:T(8,128)}, u32[]{:S(2)}, u32[]{:S(2)}) %all-to-all-start.1) | async-done | bytes 524320 | tf_op jit(solution)/shard_map/all_to_all | solution.py:46
  182.8 1.1 reduce_sum.9
  183.9 0.2 copy.7
  184.1 1.0 reshape.132
  185.1 4.2 %all-to-all-start.2 = ((f32[4,1,1024]{2,1,0:T(1,128)}), f32[4,1,1024]{2,1,0:T(1,128)S(1)}, u32[]{:S(2)}, u32[]{:S(2)}) async-start(f32[4,1,1024]{2,1,0:T(1,128)} %reshape.132), calls=%async_computation.2 | async-start | bytes 32768 | tf_op jit(solution)/shard_map/all_to_all | solution.py:87
  189.2 0.0 collective-permute-done
  189.2 0.0 collective-permute-done.1
  189.2 6.8 %fusion.6 = bf16[2,64,1,4096]{3,1,2,0:T(8,128)(2,1)} fusion(f32[2,64,1,4032]{3,1,2,0:T(8,128)} %get-tuple-element.19, f32[2,64,1,64]{3,1,2,0:T(8,128)S(1)} %get-tuple-element.21, f32[2,64,1,64]{3,1,2,0:T(8,128)S(1)} %get-tuple-element.20, f32[2,64,1,4032]{3,1,2,0:T(8,128)} %get-tuple-element.18, f32[2,64,1,63]{3,1,2,0:T(8,128)} %get-tuple-element.15, ...), kind=kLoop, calls=%fused_computation.9 | loop fusion | flops 11534336 | bytes 16801792 | tf_op jit(solution)/shard_map/convert_element_type | solution.py:63
  196.1 0.0 all-to-all-done.2
  196.1 0.5 broadcast.23
  196.6 0.7 reduce
  197.3 0.4 reshape.133
  197.7 0.7 copy.8
  (1 shorter events, 0.0 us)
Async XLA Ops:
  7.2 137.2 %all-gather.3.cloned.1.call-start = ((), (), s32[]{:S(2)}) async-start(), calls=%async_computation.3 | async-start | bytes 5242880 | tf_op jit(solution)/shard_map/all_gather | solution.py:75
  11.6 5.5 %copy-start = (bf16[2,64,1,4096]{3,1,2,0:T(8,128)(2,1)S(1)}, bf16[2,64,1,4096]{3,1,2,0:T(8,128)(2,1)}, u32[]{:S(2)}) copy-start(bf16[2,64,1,4096]{3,1,2,0:T(8,128)(2,1)} %param.2) | copy-start | bytes 3145732
  11.6 53.2 %all-to-all-start = ((bf16[4,2,64,4096]{3,2,1,0:T(8,128)(2,1)}), bf16[4,2,64,4096]{3,2,1,0:T(8,128)(2,1)}, u32[]{:S(2)}, u32[]{:S(2)}) async-start(bf16[4,2,64,4096]{3,2,1,0:T(8,128)(2,1)} %broadcast_in_dim.11), calls=%async_computation | async-start | bytes 8388608 | tf_op jit(solution)/shard_map/all_to_all | solution.py:11
  17.1 172.2 %collective-permute-start = (bf16[2,64,1,4096]{3,1,2,0:T(8,128)(2,1)S(1)}, bf16[2,64,1,4096]{3,1,2,0:T(8,128)(2,1)}, u32[]{:S(2)}, u32[]{:S(2)}) collective-permute-start(bf16[2,64,1,4096]{3,1,2,0:T(8,128)(2,1)S(1)} %copy-done), channel_id=1, source_target_pairs={{0,1},{1,2},{2,3},{3,4},{4,5},{5,6},{6,7},{7,8},{8,9},{9,10},{10,1... | collective-permute-start | bytes 3145736 | tf_op jit(solution)/shard_map/ppermute | solution.py:31
  19.0 170.2 %collective-permute-start.1 = (bf16[2,64,1,4096]{3,1,2,0:T(8,128)(2,1)S(1)}, bf16[2,64,1,4096]{3,1,2,0:T(8,128)(2,1)}, u32[]{:S(2)}, u32[]{:S(2)}) collective-permute-start(bf16[2,64,1,4096]{3,1,2,0:T(8,128)(2,1)S(1)} %copy-done), channel_id=1, source_target_pairs={{1,0},{2,1},{3,2},{4,3},{5,4},{6,5},{7,6},{8,7},{9,8},{10,9},{11,1... | collective-permute-start | bytes 3145736 | tf_op jit(solution)/shard_map/ppermute | solution.py:34
  144.4 3.1 %copy-start.2 = (bf16[1,4,64,4096]{3,2,0,1:T(8,128)(2,1)S(1)}, bf16[1,4,64,4096]{3,2,0,1:T(8,128)(2,1)}, u32[]{:S(2)}) copy-start(bf16[1,4,64,4096]{3,2,0,1:T(8,128)(2,1)} %get-tuple-element.8) | copy-start | bytes 6291460
  147.5 2.8 %copy-start.3 = (bf16[2,256,1,4096]{3,1,2,0:T(8,128)(2,1)S(1)}, bf16[2,256,1,4096]{3,1,2,0:T(8,128)(2,1)}, u32[]{:S(2)}) copy-start(bf16[2,256,1,4096]{3,1,2,0:T(8,128)(2,1)} %all-gather.3.cloned.1.call-done) | copy-start | bytes 12582916
  150.4 1.6 copy-start.1
  153.6 29.2 %all-to-all-start.1 = ((f32[32,8,512]{2,1,0:T(8,128)}), f32[32,8,512]{2,1,0:T(8,128)}, u32[]{:S(2)}, u32[]{:S(2)}) async-start(f32[32,8,512]{2,1,0:T(8,128)} %maximum_multiply_fusion), calls=%async_computation.1 | async-start | bytes 1048576 | tf_op jit(solution)/shard_map/all_to_all | solution.py:46
  185.1 11.0 %all-to-all-start.2 = ((f32[4,1,1024]{2,1,0:T(1,128)}), f32[4,1,1024]{2,1,0:T(1,128)S(1)}, u32[]{:S(2)}, u32[]{:S(2)}) async-start(f32[4,1,1024]{2,1,0:T(1,128)} %reshape.132), calls=%async_computation.2 | async-start | bytes 32768 | tf_op jit(solution)/shard_map/all_to_all | solution.py:87
Sparse Core Ops, SparseCore 0:
  10.1 134.2 all-gather.2
where the time goes:
time: 206 us; the launch traced here: 205 us
  waiting for transfers between devices  123 us (60%)
  starting transfers between devices  30.7 us (15%)
  local copies, waits for them, and re-layouts  20.6 us (10%)
  between operations  14.1 us (7%)
  other arithmetic  10.1 us (5%)
  matrix products  7.07 us (3%)
    all_gather x1, waiting for transfers between devices, shards(): panel = lax.all_gather(flat, 'col', axis=1, tiled=True)  74.9 us
    all_to_all x1, waiting for transfers between devices, sent_to_all(): return lax.all_to_all(copies, axis, split_axis=0, concat_axis=0, tiled=True)  29.5 us
    all_to_all x1, waiting for transfers between devices, sum_at_owner(): pieces = lax.all_to_all(cut_along(x, dim, size), axis, 0, 0, tiled=True)  17.6 us
    ppermute x1, starting transfers between devices, with_halo(): lax.ppermute(lax.slice_in_dim(block, 0, width, axis=dim), axis, backward)  9.96 us
    all_to_all x1, starting transfers between devices, sum_at_owner(): pieces = lax.all_to_all(cut_along(x, dim, size), axis, 0, 0, tiled=True)  9.19 us
    dot_general x4, matrix products, contract(): lax.dot_general(left, right, (((1,), (1,)), ((), ())), preferred_element_...  7.07 us
    convert_element_type x1, other arithmetic, apply_operator(): return (-0.5 * lap + potential[None, None] * center).astype(jnp.bfloat16)  6.82 us
    all_to_all x1, starting transfers between devices, sent_to_all(): return lax.all_to_all(copies, axis, split_axis=0, concat_axis=0, tiled=True)  5.47 us
  transfers between devices with their start and end apart: 6, of which 3 were waited for; matrix products, arithmetic and copies ran while one was open for 17% of the time, Pallas kernels for 0%

commit v1 on v0

--- a/solution.py
+++ b/solution.py
@@ -72,7 +72,10 @@
 def shards(orbitals, potential):
     parts, orbs, planes, cells = orbitals.shape
     flat = orbitals.reshape(parts, orbs, planes * cells)
-    panel = lax.all_gather(flat, "col", axis=1, tiled=True)
+    count_2 = lax.axis_size("col")
+    blocks = jnp.stack([flat for _ in range(count_2)])
+    blocks = lax.all_to_all(blocks, "col", split_axis=0, concat_axis=0)
+    panel = jnp.concatenate(blocks, axis=1)
     other = gathered_copies(flat, "row", 1)
     padded = with_halo(orbitals, (("depth", 2),), 1)
     applied = apply_operator(padded, potential)

time: 206 us -> 259 us (1.26)
  the two profiles are of different devices: /device:TPU:10 before, /device:TPU:8 now
where the time goes in v1:
time: 259 us; the launch traced here: 258 us
  waiting for transfers between devices  134 us (52%)
  blocking collectives  53 us (20%)
  starting transfers between devices  35 us (14%)
  local copies, waits for them, and re-layouts  21.9 us (8%)
  other arithmetic  10.1 us (4%)
  matrix products  2.96 us (1%)
    all_to_all x1, waiting for transfers between devices, shards(): blocks = lax.all_to_all(blocks, 'col', split_axis=0, concat_axis=0)  117 us
    all_to_all x1, blocking collectives, sent_to_all(): return lax.all_to_all(copies, axis, split_axis=0, concat_axis=0, tiled=True)  53 us
    all_to_all x1, waiting for transfers between devices, sum_at_owner(): pieces = lax.all_to_all(cut_along(x, dim, size), axis, 0, 0, tiled=True)  17.6 us
    all_to_all x1, starting transfers between devices, sum_at_owner(): pieces = lax.all_to_all(cut_along(x, dim, size), axis, 0, 0, tiled=True)  14 us
    ppermute x1, starting transfers between devices, with_halo(): lax.ppermute(lax.slice_in_dim(block, 0, width, axis=dim), axis, backward)  8.45 us
    all_to_all x1, starting transfers between devices, shards(): blocks = lax.all_to_all(blocks, 'col', split_axis=0, concat_axis=0)  7.39 us
    convert_element_type x1, other arithmetic, apply_operator(): return (-0.5 * lap + potential[None, None] * center).astype(jnp.bfloat16)  6.82 us
    unnamed x13, local copies, waits for them, and re-layouts  6.03 us
  transfers between devices with their start and end apart: 5, of which 2 were waited for; matrix products, arithmetic and copies ran while one was open for 10% of the time, Pallas kernels for 0%

profile of v1, /device:TPU:8, one launch (start us, length us, event | category | flops | bytes accessed | tf_op | source)
XLA Modules:
  0.0 258.0 jit_solution(11956113015463955618)
XLA Ops:
  0.6 1.7 stack.3
  2.4 0.0 copy-start.1
  2.4 2.0 copy-done.1
  4.3 53.0 %all_to_all.20 = bf16[4,2,64,4096]{3,2,1,0:T(8,128)(2,1)} all-to-all(bf16[4,2,64,4096]{3,2,1,0:T(8,128)(2,1)S(1)} %stack.3), channel_id=1, replica_groups=mesh['row'=4,'col'=4,'depth'=32] {'row'}, dimensions={0} | all-to-all | bytes 8388608 | tf_op jit(solution)/shard_map/all_to_all | solution.py:11
  57.3 0.0 copy-start
  57.3 7.4 %all-to-all-start = ((bf16[4,2,64,4096]{3,2,1,0:T(8,128)(2,1)}), bf16[4,2,64,4096]{3,2,1,0:T(8,128)(2,1)}, u32[]{:S(2)}, u32[]{:S(2)}) async-start(bf16[4,2,64,4096]{3,2,1,0:T(8,128)(2,1)} %copy-done.1), calls=%async_computation | async-start | bytes 8388608 | tf_op jit(solution)/shard_map/all_to_all | solution.py:77
  64.7 0.0 copy-done
  64.7 1.9 collective-permute-start
  66.6 8.4 %collective-permute-start.1 = (bf16[2,64,1,4096]{3,1,2,0:T(8,128)(2,1)S(1)}, bf16[2,64,1,4096]{3,1,2,0:T(8,128)(2,1)}, u32[]{:S(2)}, u32[]{:S(2)}) collective-permute-start(bf16[2,64,1,4096]{3,1,2,0:T(8,128)(2,1)S(1)} %copy-done), channel_id=1, source_target_pairs={{1,0},{2,1},{3,2},{4,3},{5,4},{6,5},{7,6},{8,7},{9,8},{10,9},{11,1... | collective-permute-start | bytes 3145736 | tf_op jit(solution)/shard_map/ppermute | solution.py:34
  75.1 0.6 fusion.11
  75.7 0.1 fusion.21
  75.8 0.7 fusion.18
  76.5 0.7 fusion.17
  77.2 2.4 fusion.19
  79.6 0.0 copy-start.3
  79.6 2.6 %fusion.20 = (f32[2,64,1,4032]{3,1,2,0:T(8,128)}, f32[2,64,1,4032]{3,1,2,0:T(8,128)}) fusion(bf16[2,64,1,4096]{3,1,2,0:T(8,128)(2,1)S(1)} %copy-done), kind=kLoop, calls=%fused_computation.28 | loop fusion | bytes 8257536 | tf_op jit(solution)/shard_map/jit(_roll_static)/slice | solution.py:57
  82.2 1.1 copy-done.3
  83.3 1.8 fusion.14
  85.1 116.7 %all-to-all-done = bf16[4,2,64,4096]{3,2,1,0:T(8,128)(2,1)} async-done(((bf16[4,2,64,4096]{3,2,1,0:T(8,128)(2,1)}), bf16[4,2,64,4096]{3,2,1,0:T(8,128)(2,1)}, u32[]{:S(2)}, u32[]{:S(2)}) %all-to-all-start) | async-done | bytes 4194336 | tf_op jit(solution)/shard_map/all_to_all | solution.py:77
  201.8 2.7 %fusion.15 = (bf16[1,4,64,4096]{3,2,0,1:T(8,128)(2,1)S(1)}, bf16[1,4,64,4096]{3,2,0,1:T(8,128)(2,1)S(1)}) fusion(bf16[2,4,64,4096]{3,2,0,1:T(8,128)(2,1)} %bitcast.1), kind=kLoop, calls=%fused_computation.23 | loop fusion | bytes 8388608 | tf_op jit(solution)/shard_map/slice | solution.py:85
  204.5 0.0 copy-start.2
  204.5 0.7 fusion.23
  205.2 0.8 copy-done.2
  206.1 0.7 fusion.22
  206.8 0.7 fusion.7
  207.6 0.7 fusion.8
  208.3 0.9 maximum_multiply_fusion
  209.2 14.0 %all-to-all-start.2 = ((f32[32,8,512]{2,1,0:T(8,128)}), f32[32,8,512]{2,1,0:T(8,128)}, u32[]{:S(2)}, u32[]{:S(2)}) async-start(f32[32,8,512]{2,1,0:T(8,128)} %maximum_multiply_fusion), calls=%async_computation.2 | async-start | bytes 1048576 | tf_op jit(solution)/shard_map/all_to_all | solution.py:46
  223.2 0.0 copy-start.4
  223.2 2.4 fusion.16
  225.7 17.6 %all-to-all-done.2 = f32[32,8,512]{2,1,0:T(8,128)} async-done(((f32[32,8,512]{2,1,0:T(8,128)}), f32[32,8,512]{2,1,0:T(8,128)}, u32[]{:S(2)}, u32[]{:S(2)}) %all-to-all-start.2) | async-done | bytes 524320 | tf_op jit(solution)/shard_map/all_to_all | solution.py:46
  243.3 1.1 reduce_sum.9
  244.4 0.2 copy.7
  244.5 1.0 reshape.135
  245.5 3.3 %all-to-all-start.3 = ((f32[4,1,1024]{2,1,0:T(1,128)}), f32[4,1,1024]{2,1,0:T(1,128)S(1)}, u32[]{:S(2)}, u32[]{:S(2)}) async-start(f32[4,1,1024]{2,1,0:T(1,128)} %reshape.135), calls=%async_computation.3 | async-start | bytes 32768 | tf_op jit(solution)/shard_map/all_to_all | solution.py:90
  248.8 0.0 collective-permute-done
  248.8 0.0 collective-permute-done.1
  248.8 0.0 copy-done.4
  248.8 6.8 %fusion.6 = bf16[2,64,1,4096]{3,1,2,0:T(8,128)(2,1)} fusion(f32[2,64,1,4032]{3,1,2,0:T(8,128)} %get-tuple-element.21, f32[2,64,1,64]{3,1,2,0:T(8,128)S(1)} %get-tuple-element.23, f32[2,64,1,64]{3,1,2,0:T(8,128)S(1)} %get-tuple-element.22, f32[2,64,1,4032]{3,1,2,0:T(8,128)} %get-tuple-element.20, f32[2,64,1,63]{3,1,2,0:T(8,128)} %get-tuple-element.17, ...), kind=kLoop, calls=%fused_computation.7 | loop fusion | flops 11534336 | bytes 16801792 | tf_op jit(solution)/shard_map/convert_element_type | solution.py:63
  255.6 0.0 all-to-all-done.3
  255.7 0.5 broadcast.24
  256.2 0.7 reduce
  256.9 0.4 reshape.136
  257.3 0.7 copy.8
  (1 shorter events, 0.0 us)
Async XLA Ops:
  2.4 2.0 copy-start.1
  57.3 7.4 %copy-start = (bf16[2,64,1,4096]{3,1,2,0:T(8,128)(2,1)S(1)}, bf16[2,64,1,4096]{3,1,2,0:T(8,128)(2,1)}, u32[]{:S(2)}) copy-start(bf16[2,64,1,4096]{3,1,2,0:T(8,128)(2,1)} %param.2) | copy-start | bytes 3145732
  57.3 144.4 %all-to-all-start = ((bf16[4,2,64,4096]{3,2,1,0:T(8,128)(2,1)}), bf16[4,2,64,4096]{3,2,1,0:T(8,128)(2,1)}, u32[]{:S(2)}, u32[]{:S(2)}) async-start(bf16[4,2,64,4096]{3,2,1,0:T(8,128)(2,1)} %copy-done.1), calls=%async_computation | async-start | bytes 8388608 | tf_op jit(solution)/shard_map/all_to_all | solution.py:77
  64.7 184.1 %collective-permute-start = (bf16[2,64,1,4096]{3,1,2,0:T(8,128)(2,1)S(1)}, bf16[2,64,1,4096]{3,1,2,0:T(8,128)(2,1)}, u32[]{:S(2)}, u32[]{:S(2)}) collective-permute-start(bf16[2,64,1,4096]{3,1,2,0:T(8,128)(2,1)S(1)} %copy-done), channel_id=1, source_target_pairs={{0,1},{1,2},{2,3},{3,4},{4,5},{5,6},{6,7},{7,8},{8,9},{9,10},{10,1... | collective-permute-start | bytes 3145736 | tf_op jit(solution)/shard_map/ppermute | solution.py:31
  66.6 182.2 %collective-permute-start.1 = (bf16[2,64,1,4096]{3,1,2,0:T(8,128)(2,1)S(1)}, bf16[2,64,1,4096]{3,1,2,0:T(8,128)(2,1)}, u32[]{:S(2)}, u32[]{:S(2)}) collective-permute-start(bf16[2,64,1,4096]{3,1,2,0:T(8,128)(2,1)S(1)} %copy-done), channel_id=1, source_target_pairs={{1,0},{2,1},{3,2},{4,3},{5,4},{6,5},{7,6},{8,7},{9,8},{10,9},{11,1... | collective-permute-start | bytes 3145736 | tf_op jit(solution)/shard_map/ppermute | solution.py:34
  79.6 3.7 %copy-start.3 = (bf16[4,2,64,4096]{3,2,1,0:T(8,128)(2,1)S(1)}, bf16[4,2,64,4096]{3,2,1,0:T(8,128)(2,1)}, u32[]{:S(2)}) copy-start(bf16[4,2,64,4096]{3,2,1,0:T(8,128)(2,1)} %all_to_all.20) | copy-start | bytes 12582916
  204.5 1.6 copy-start.2
  209.2 34.1 %all-to-all-start.2 = ((f32[32,8,512]{2,1,0:T(8,128)}), f32[32,8,512]{2,1,0:T(8,128)}, u32[]{:S(2)}, u32[]{:S(2)}) async-start(f32[32,8,512]{2,1,0:T(8,128)} %maximum_multiply_fusion), calls=%async_computation.2 | async-start | bytes 1048576 | tf_op jit(solution)/shard_map/all_to_all | solution.py:46
  223.2 25.6 %copy-start.4 = (f32[2,64,1,4033]{3,1,2,0:T(8,128)S(1)}, f32[2,64,1,4033]{3,1,2,0:T(8,128)}, u32[]{:S(2)}) copy-start(f32[2,64,1,4033]{3,1,2,0:T(8,128)} %get-tuple-element.18) | copy-start | bytes 6194692
  245.5 10.1 %all-to-all-start.3 = ((f32[4,1,1024]{2,1,0:T(1,128)}), f32[4,1,1024]{2,1,0:T(1,128)S(1)}, u32[]{:S(2)}, u32[]{:S(2)}) async-start(f32[4,1,1024]{2,1,0:T(1,128)} %reshape.135), calls=%async_computation.3 | async-start | bytes 32768 | tf_op jit(solution)/shard_map/all_to_all | solution.py:90
